TPU v7x, 32 devices: a whole 2x2x4 slice. The times are simulated.
32 devices in a mesh: seq: 8 (over z, x), tp: 4 (over y, core).
Axes of the slice: x: 2, y: 2, z: 4, core: 2. Of those that a mesh axis runs over, the one named last changes fastest.
Arguments:
- queries: bfloat16 [2048, 8192], P('seq', 'tp'), may hold values from -120 to 120
- keys: bfloat16 [2048, 1024], P('seq', 'tp'), may hold values from -5 to 5
- values: bfloat16 [2048, 1024], P('seq', 'tp'), may hold values from -6 to 6
- w_query: bfloat16 [8192, 8192], P('seq', 'tp'), may hold values from -0.0625 to 0.0625
- key_weight: bfloat16 [8192, 1024], P('seq'), may hold values from -0.0625 to 0.0625
Outputs:
- attended: bfloat16 [2048, 8192], P('seq', 'tp')
- head_logit_maxima: float32 [64], P('tp')
- w_query_clipped: bfloat16 [8192, 8192], P('seq', 'tp')
- clipped_key_weight: bfloat16 [8192, 1024], P('seq')
All inputs are finite; a program needn't handle non-finite values.
Results may differ from a plain program's by a relative error of at most 0.004.
Values may be sent and summed in bfloat16 or wider, within the bound.
A program may use at most 64 MiB of HBM per device.

v0:
```python
import functools
import math

import jax
import jax.numpy as jnp
from jax import lax
from jax.experimental import pallas as pl
from jax.experimental.pallas import tpu as pltpu
from jax.sharding import PartitionSpec as P

HEAD_SIZE = 128
LANES = 128

clip_threshold = 10.0
HEADS_PER_STEP = 8
MESH = pl.DeviceIdType.MESH


def grid_of(n):
    columns = max(d for d in range(1, n + 1) if n % d == 0 and d * d <= n)
    return n // columns, columns


def attend_kernel(
    n, tp_n, heads, kv_heads, rows,
    q_hbm, k_hbm, v_hbm,
    o_hbm, qf_ref, kf_ref, hm_ref,
    qv, kb, vb, kt, acc, mrun, ob, mxl, mxb, gml, gmb,
    lq, lkv, lo, k_recv, v_recv, k_send, v_send, mx_recv, mx_send, gm_recv, gm_send,
):
    group = heads // kv_heads
    nz, nx = grid_of(n)
    me = lax.axis_index("seq")
    tp = lax.axis_index("tp")
    z, x = lax.div(me, nx), lax.rem(me, nx)

    def head_cols(h):
        return pl.ds(h * HEAD_SIZE, HEAD_SIZE)

    kv_copies = []
    for g in range(kv_heads):
        kv_copies.append(pltpu.make_async_copy(k_hbm.at[:, head_cols(g)], kb.at[me, g], lkv.at[0, g]))
        kv_copies.append(pltpu.make_async_copy(v_hbm.at[:, head_cols(g)], vb.at[me, g], lkv.at[1, g]))
    for copy in kv_copies:
        copy.start()
    q_copies = [
        pltpu.make_async_copy(q_hbm.at[:, head_cols(h)], qv.at[h], lq.at[h]) for h in range(heads)
    ]
    for copy in q_copies:
        copy.start()

    barrier = pltpu.get_barrier_semaphore()
    for d in range(1, n):
        pl.semaphore_signal(
            barrier, inc=1, device_id={"seq": lax.rem(me + d, n)}, device_id_type=MESH
        )
    for d in range(1, tp_n):
        pl.semaphore_signal(
            barrier, inc=1, device_id={"tp": lax.rem(tp + d, tp_n)}, device_id_type=MESH
        )
    for copy in kv_copies:
        copy.wait()
    pl.semaphore_wait(barrier, n - 1 + tp_n - 1)

    def piece(kind, block, way, target):
        buf, send, recv = ((kb, k_send, k_recv), (vb, v_send, v_recv))[kind]
        return pltpu.make_async_remote_copy(
            src_ref=buf.at[block], dst_ref=buf.at[block],
            send_sem=send.at[way, block], recv_sem=recv.at[block],
            device_id={"seq": target}, device_id_type=MESH,
        )

    def each_send(kind, row, col, act):
        block = row * nx + col

        @pl.when((col == x) & (z + 1 < nz))
        def _():
            act(piece(kind, block, 0, lax.rem(me + nx, n)))

        @pl.when((col <= x) & (x + 1 < nx))
        def _():
            act(piece(kind, block, 1, lax.rem(me + 1, n)))

        @pl.when((col >= x) & (x > 0) & (row < z))
        def _():
            act(piece(kind, block, 2, lax.rem(me + n - 1, n)))

    start = lambda copy: copy.start()
    for kind in range(2):
        each_send(kind, z, x, start)
    for copy in q_copies:
        copy.wait()

    scale = HEAD_SIZE ** (-0.5)
    to_exp2 = scale * math.log2(math.e)
    ones = jnp.ones((rows, LANES), jnp.bfloat16)

    def wide(a):
        return jnp.concatenate([a] * (rows // LANES), axis=1)

    def widest(s):
        top = s[:, :LANES]
        for i in range(1, rows // LANES):
            top = jnp.maximum(top, s[:, i * LANES:(i + 1) * LANES])
        return jnp.broadcast_to(jnp.max(top, axis=1, keepdims=True), (rows, LANES))

    steps = heads // HEADS_PER_STEP

    def place(t):
        u = jnp.maximum(t - x - 1, 0)
        first = t <= x
        w = jnp.maximum(u - 1, 0)
        k = 1 + lax.div(w, nx)
        j = lax.rem(w, nx) + jnp.where(k == z, 1, 0)
        up = jnp.where(u == 0, 1, jnp.where(j == 0, k + 1, k))
        left = jnp.where(u == 0, 0, j)
        row = jnp.where(first, z, z - up)
        col = jnp.where(first, x - t, lax.rem(x + nx - left, nx))
        return row, col

    def take(kind, t):
        row, col = place(t)
        piece(kind, row * nx + col, 0, lax.rem(me + 1, n)).wait_recv()
        each_send(kind, row, col, start)

    def attend(block, t, own):
        for g in range(kv_heads):
            kt[g] = kb[block, g].T

        @pl.loop(0, steps)
        def _(step):
            for i in range(HEADS_PER_STEP):
                h = step * HEADS_PER_STEP + i
                g = lax.div(h, group)
                s = jnp.dot(qv[h], kt[g], preferred_element_type=jnp.float32)
                if own:
                    r = lax.broadcasted_iota(jnp.int32, (rows, rows), 0)
                    c = lax.broadcasted_iota(jnp.int32, (rows, rows), 1)
                    s = jnp.where(r >= c, s, jnp.float32(-1e30))
                v_ones = jnp.concatenate([vb[block, g], ones], axis=1)
                if own:
                    top = widest(s)
                    p = jnp.exp2((s - wide(top)) * to_exp2).astype(jnp.bfloat16)
                    acc[h] = jnp.dot(p, v_ones, preferred_element_type=jnp.float32)
                else:
                    old = mrun[h]
                    top = jnp.maximum(old, widest(s))
                    p = jnp.exp2((s - wide(top)) * to_exp2).astype(jnp.bfloat16)
                    keep = jnp.exp2((old - top) * to_exp2)
                    acc[h] = acc[h] * jnp.concatenate([keep, keep], axis=1) + jnp.dot(
                        p, v_ones, preferred_element_type=jnp.float32
                    )
                mrun[h] = top

            @pl.when((step == steps // 2 - 1) & (t < me))
            def _():
                take(0, t + 1)

            @pl.when((step == steps - 1) & (t < me))
            def _():
                take(1, t + 1)

    attend(me, 0, True)

    def one_block(t, carry):
        row, col = place(t)
        attend(row * nx + col, t, False)
        return carry

    lax.fori_loop(1, me + 1, one_block, 0)

    sub = lax.broadcasted_iota(jnp.int32, (heads, LANES), 0)
    local = jnp.zeros((heads, LANES), jnp.float32)
    for h in range(heads):
        local = jnp.where(sub == h, jnp.max(mrun[h], axis=0, keepdims=True), local)
    mxl[...] = local

    def mx_copy(d):
        return pltpu.make_async_remote_copy(
            src_ref=mxl, dst_ref=mxb.at[d - 1], send_sem=mx_send.at[d - 1],
            recv_sem=mx_recv.at[d - 1], device_id={"seq": lax.rem(me + d, n)}, device_id_type=MESH,
        )

    for d in range(1, n):
        mx_copy(d).start()

    for h in range(heads):
        a = acc[h]
        ob[h] = (a[:, :HEAD_SIZE] / a[:, HEAD_SIZE:]).astype(jnp.bfloat16)
        pltpu.make_async_copy(ob.at[h], o_hbm.at[:, head_cols(h)], lo.at[h]).start()

    top = local
    for d in range(1, n):
        mx_copy(d).wait_recv()
        top = jnp.maximum(top, mxb[d - 1])
    top = top * scale
    gsub = lax.broadcasted_iota(jnp.int32, (8, LANES), 0)
    gtop = jnp.zeros((8, LANES), jnp.float32)
    for g in range(kv_heads):
        gtop = jnp.where(
            gsub == g, jnp.max(top[g * group:(g + 1) * group], axis=0, keepdims=True), gtop
        )
    gml[...] = gtop

    def gm_copy(d):
        return pltpu.make_async_remote_copy(
            src_ref=gml, dst_ref=gmb.at[d - 1], send_sem=gm_send.at[d - 1],
            recv_sem=gm_recv.at[d - 1], device_id={"tp": lax.rem(tp + d, tp_n)}, device_id_type=MESH,
        )

    for d in range(1, tp_n):
        gm_copy(d).start()

    lane = lax.broadcasted_iota(jnp.int32, (1, LANES), 1)
    hm = jnp.zeros((1, LANES), jnp.float32)
    gamma = clip_threshold / jnp.maximum(top, clip_threshold)
    clip = clip_threshold / jnp.maximum(gtop, clip_threshold)
    for h in range(heads):
        hm = jnp.where(lane == h, top[h:h + 1], hm)
        g = h // group
        qf_ref[:, h * HEAD_SIZE:(h + 1) * HEAD_SIZE] = gamma[h:h + 1] / jnp.sqrt(clip[g:g + 1])
    hm_ref[...] = hm

    def put_key_factors(owner, factors):
        for g in range(kv_heads):
            at = pl.multiple_of((owner * kv_heads + g) * HEAD_SIZE, HEAD_SIZE)
            kf_ref[:, pl.ds(at, HEAD_SIZE)] = jnp.sqrt(factors[g:g + 1])

    put_key_factors(tp, clip)
    for d in range(1, tp_n):
        gm_copy(d).wait_recv()
        put_key_factors(
            lax.rem(tp + tp_n - d, tp_n), clip_threshold / jnp.maximum(gmb[d - 1], clip_threshold)
        )

    def sent_row(row, carry):
        def sent_col(col, carry):
            @pl.when((row < z) | (col <= x))
            def _():
                for kind in range(2):
                    each_send(kind, row, col, lambda copy: copy.wait_send())

            return carry

        return lax.fori_loop(0, nx, sent_col, carry)

    lax.fori_loop(0, z + 1, sent_row, 0)
    for d in range(1, n):
        mx_copy(d).wait_send()
    for d in range(1, tp_n):
        gm_copy(d).wait_send()
    for h in range(heads):
        pltpu.make_async_copy(ob.at[h], o_hbm.at[:, head_cols(h)], lo.at[h]).wait()


def shards(n, tp_n, queries, keys, values, w_query, key_weight):
    rows = queries.shape[0]
    heads = queries.shape[1] // HEAD_SIZE
    kv_heads = keys.shape[1] // HEAD_SIZE
    any_space = pl.BlockSpec(memory_space=pl.ANY)
    vmem = pl.BlockSpec(memory_space=pltpu.VMEM)
    dma = pltpu.SemaphoreType.DMA
    attended, q_factor, k_factor, maxima = pl.pallas_call(
        functools.partial(attend_kernel, n, tp_n, heads, kv_heads, rows),
        name="attend",
        out_shape=(
            jax.ShapeDtypeStruct(queries.shape, jnp.bfloat16),
            jax.ShapeDtypeStruct((1, heads * HEAD_SIZE), jnp.float32),
            jax.ShapeDtypeStruct((1, key_weight.shape[1]), jnp.float32),
            jax.ShapeDtypeStruct((1, LANES), jnp.float32),
        ),
        in_specs=[pl.BlockSpec(memory_space=pltpu.HBM)] * 3,
        out_specs=(any_space, vmem, vmem, vmem),
        scratch_shapes=[
            pltpu.VMEM((heads, rows, HEAD_SIZE), jnp.bfloat16),
            pltpu.VMEM((n, kv_heads, rows, HEAD_SIZE), jnp.bfloat16),
            pltpu.VMEM((n, kv_heads, rows, HEAD_SIZE), jnp.bfloat16),
            pltpu.VMEM((kv_heads, HEAD_SIZE, rows), jnp.bfloat16),
            pltpu.VMEM((heads, rows, 2 * HEAD_SIZE), jnp.float32),
            pltpu.VMEM((heads, rows, LANES), jnp.float32),
            pltpu.VMEM((heads, rows, HEAD_SIZE), jnp.bfloat16),
            pltpu.VMEM((heads, LANES), jnp.float32),
            pltpu.VMEM((n - 1, heads, LANES), jnp.float32),
            pltpu.VMEM((8, LANES), jnp.float32),
            pltpu.VMEM((tp_n - 1, 8, LANES), jnp.float32),
            dma((heads,)),
            dma((2, kv_heads)),
            dma((heads,)),
            dma((n,)),
            dma((n,)),
            dma((3, n)),
            dma((3, n)),
            dma((n - 1,)),
            dma((n - 1,)),
            dma((tp_n - 1,)),
            dma((tp_n - 1,)),
        ],
        compiler_params=pltpu.CompilerParams(
            collective_id=0, has_side_effects=True, vmem_limit_bytes=32 * 1024 * 1024
        ),
        cost_estimate=pl.CostEstimate(
            flops=4 * rows * rows * n * heads * HEAD_SIZE,
            bytes_accessed=4 * rows * heads * HEAD_SIZE,
            transcendentals=rows * rows * n * heads,
        ),
    )(*(pltpu.with_memory_space_constraint(a, pltpu.HBM) for a in (queries, keys, values)))
    w_query_clipped = (w_query.astype(jnp.float32) * q_factor).astype(jnp.bfloat16)
    clipped_key_weight = (key_weight.astype(jnp.float32) * k_factor).astype(jnp.bfloat16)
    return attended, maxima[0, :heads], w_query_clipped, clipped_key_weight


def solution(mesh):
    in_specs = (P("seq", "tp"), P("seq", "tp"), P("seq", "tp"), P("seq", "tp"), P("seq", None))
    out_specs = (P("seq", "tp"), P("tp"), P("seq", "tp"), P("seq", None))
    body = functools.partial(shards, mesh.shape["seq"], mesh.shape["tp"])
    return jax.shard_map(body, mesh=mesh, in_specs=in_specs, out_specs=out_specs, check_vma=False)
```

profile of v0, /device:TPU:0, one launch (start us, length us, event | category | flops | bytes accessed | tf_op | source)
XLA Modules:
  0.0 48.5 jit_solution(4193352812194764922)
XLA Ops:
  0.6 0.0 copy-start
  0.6 41.3 %attend.1 = (bf16[256,2048]{1,0:T(8,128)(2,1)S(1)}, f32[1,2048]{1,0:T(1,128)S(1)}, f32[1,1024]{1,0:T(1,128)S(1)}, f32[1,128]{1,0:T(1,128)S(1)}) custom-call(bf16[256,2048]{1,0:T(8,128)(2,1)} %q_hbm.1, bf16[256,256]{1,0:T(8,128)(2,1)} %k_hbm.1, bf16[256,256]{1,0:T(8,128)(2,1)} %v_hbm.1), custom_call_target="tpu_custom_call" | custom-call | flops 4294967296 | bytes 2097152 | tf_op jit(solution)/shard_map/attend/pallas_call | solution.py:263
  42.0 0.5 %slice_bitcast_fusion = f32[16]{0:T(128)} fusion(f32[1,128]{1,0:T(1,128)S(1)} %get-tuple-element.9), kind=kLoop, calls=%fused_computation.2 | loop fusion | bytes 128 | tf_op jit(solution)/shard_map/squeeze | solution.py:309
  42.5 0.0 copy-done
  42.5 0.0 copy-start.1
  42.5 3.2 %multiply_convert_fusion = bf16[1024,2048]{1,0:T(8,128)(2,1)} fusion(bf16[1024,2048]{1,0:T(8,128)(2,1)S(1)} %copy-done, f32[2048]{0:T(1024)S(1)} %bitcast.4), kind=kLoop, calls=%fused_computation | loop fusion | flops 6291456 | bytes 8396800 | tf_op jit(solution)/shard_map/convert_element_type | solution.py:307
  45.6 0.0 copy-done.1
  45.6 1.9 %multiply_convert_fusion.1 = bf16[1024,1024]{1,0:T(8,128)(2,1)} fusion(bf16[1024,1024]{1,0:T(8,128)(2,1)S(1)} %copy-done.1, f32[1024]{0:T(1024)S(1)} %bitcast.5), kind=kLoop, calls=%fused_computation.1 | loop fusion | flops 3145728 | bytes 4198400 | tf_op jit(solution)/shard_map/convert_element_type | solution.py:308
  47.5 1.0 %copy.10 = bf16[256,2048]{1,0:T(8,128)(2,1)} copy(bf16[256,2048]{1,0:T(8,128)(2,1)S(1)} %get-tuple-element.16) | data formatting | bytes 2097152
Async XLA Ops:
  0.6 41.8 %copy-start = (bf16[1024,2048]{1,0:T(8,128)(2,1)S(1)}, bf16[1024,2048]{1,0:T(8,128)(2,1)}, u32[]{:S(2)}) copy-start(bf16[1024,2048]{1,0:T(8,128)(2,1)} %param.8) | copy-start | bytes 12582916
  42.5 3.2 %copy-start.1 = (bf16[1024,1024]{1,0:T(8,128)(2,1)S(1)}, bf16[1024,1024]{1,0:T(8,128)(2,1)}, u32[]{:S(2)}) copy-start(bf16[1024,1024]{1,0:T(8,128)(2,1)} %param.9) | copy-start | bytes 6291460
where the time goes:
time: 48.6 us; the launch traced here: 48.5 us
  Pallas kernels  41.3 us (85%)
  other arithmetic  5.04 us (10%)
  local copies, waits for them, and re-layouts  1.49 us (3%)
  between operations  0.65 us (1%)
    pallas_call x1, Pallas kernels, shards(): pl.pallas_call(functools.partial(attend_kernel, n, tp_n, heads, kv_heads,...  41.3 us
    convert_element_type x1, other arithmetic, shards(): (w_query.astype(jnp.float32) * q_factor).astype(jnp.bfloat16)  3.17 us
    convert_element_type x1, other arithmetic, shards(): (key_weight.astype(jnp.float32) * k_factor).astype(jnp.bfloat16)  1.88 us
    unnamed x5, local copies, waits for them, and re-layouts  0.98 us

commit v1 on v0

--- a/solution.py
+++ b/solution.py
@@ -24,9 +24,9 @@
 def attend_kernel(
     n, tp_n, heads, kv_heads, rows,
     q_hbm, k_hbm, v_hbm,
-    o_hbm, qf_ref, kf_ref, hm_ref,
-    qv, kb, vb, kt, acc, mrun, ob, mxl, mxb, gml, gmb,
-    lq, lkv, lo, k_recv, v_recv, k_send, v_send, mx_recv, mx_send, gm_recv, gm_send,
+    o_ref, qf_ref, kf_ref, hm_ref,
+    qv, kb, vb, kt, acc, mrun, mxl, mxb, gml, gmb,
+    lq, lkv, k_recv, v_recv, k_send, v_send, mx_recv, mx_send, gm_recv, gm_send,
 ):
     group = heads // kv_heads
     nz, nx = grid_of(n)
@@ -186,8 +186,7 @@
 
     for h in range(heads):
         a = acc[h]
-        ob[h] = (a[:, :HEAD_SIZE] / a[:, HEAD_SIZE:]).astype(jnp.bfloat16)
-        pltpu.make_async_copy(ob.at[h], o_hbm.at[:, head_cols(h)], lo.at[h]).start()
+        o_ref[:, h * HEAD_SIZE:(h + 1) * HEAD_SIZE] = (a[:, :HEAD_SIZE] / a[:, HEAD_SIZE:]).astype(jnp.bfloat16)
 
     top = local
     for d in range(1, n):
@@ -249,15 +248,31 @@
         mx_copy(d).wait_send()
     for d in range(1, tp_n):
         gm_copy(d).wait_send()
-    for h in range(heads):
-        pltpu.make_async_copy(ob.at[h], o_hbm.at[:, head_cols(h)], lo.at[h]).wait()
+
+
+CHUNKS = 8
+
+
+def finish_kernel(heads, a_ref, qf_ref, kf_ref, hm_ref, w_ref, kw_ref, a_hbm, top_ref, w_hbm, kw_hbm, wb, kwb, sem):
+    copies = [pltpu.make_async_copy(a_ref, a_hbm, sem.at[0])]
+    copies[0].start()
+    for src, factor, buf, dst, first in ((w_ref, qf_ref, wb, w_hbm, 1), (kw_ref, kf_ref, kwb, kw_hbm, 1 + CHUNKS)):
+        size = src.shape[0] // CHUNKS
+        for i in range(CHUNKS):
+            rows = pl.ds(i * size, size)
+            buf[rows, :] = (src[rows, :].astype(jnp.float32) * factor[...]).astype(jnp.bfloat16)
+            copy = pltpu.make_async_copy(buf.at[rows], dst.at[rows], sem.at[first + i])
+            copy.start()
+            copies.append(copy)
+    top_ref[...] = hm_ref[0, :heads]
+    for copy in copies:
+        copy.wait()
 
 
 def shards(n, tp_n, queries, keys, values, w_query, key_weight):
     rows = queries.shape[0]
     heads = queries.shape[1] // HEAD_SIZE
     kv_heads = keys.shape[1] // HEAD_SIZE
-    any_space = pl.BlockSpec(memory_space=pl.ANY)
     vmem = pl.BlockSpec(memory_space=pltpu.VMEM)
     dma = pltpu.SemaphoreType.DMA
     attended, q_factor, k_factor, maxima = pl.pallas_call(
@@ -270,7 +285,7 @@
             jax.ShapeDtypeStruct((1, LANES), jnp.float32),
         ),
         in_specs=[pl.BlockSpec(memory_space=pltpu.HBM)] * 3,
-        out_specs=(any_space, vmem, vmem, vmem),
+        out_specs=(vmem, vmem, vmem, vmem),
         scratch_shapes=[
             pltpu.VMEM((heads, rows, HEAD_SIZE), jnp.bfloat16),
             pltpu.VMEM((n, kv_heads, rows, HEAD_SIZE), jnp.bfloat16),
@@ -278,14 +293,12 @@
             pltpu.VMEM((kv_heads, HEAD_SIZE, rows), jnp.bfloat16),
             pltpu.VMEM((heads, rows, 2 * HEAD_SIZE), jnp.float32),
             pltpu.VMEM((heads, rows, LANES), jnp.float32),
-            pltpu.VMEM((heads, rows, HEAD_SIZE), jnp.bfloat16),
             pltpu.VMEM((heads, LANES), jnp.float32),
             pltpu.VMEM((n - 1, heads, LANES), jnp.float32),
             pltpu.VMEM((8, LANES), jnp.float32),
             pltpu.VMEM((tp_n - 1, 8, LANES), jnp.float32),
             dma((heads,)),
             dma((2, kv_heads)),
-            dma((heads,)),
             dma((n,)),
             dma((n,)),
             dma((3, n)),
@@ -304,9 +317,30 @@
             transcendentals=rows * rows * n * heads,
         ),
     )(*(pltpu.with_memory_space_constraint(a, pltpu.HBM) for a in (queries, keys, values)))
-    w_query_clipped = (w_query.astype(jnp.float32) * q_factor).astype(jnp.bfloat16)
-    clipped_key_weight = (key_weight.astype(jnp.float32) * k_factor).astype(jnp.bfloat16)
-    return attended, maxima[0, :heads], w_query_clipped, clipped_key_weight
+    hbm = pl.BlockSpec(memory_space=pltpu.HBM)
+    return pl.pallas_call(
+        functools.partial(finish_kernel, heads),
+        name="finish",
+        out_shape=(
+            jax.ShapeDtypeStruct(queries.shape, jnp.bfloat16),
+            jax.ShapeDtypeStruct((heads,), jnp.float32),
+            jax.ShapeDtypeStruct(w_query.shape, jnp.bfloat16),
+            jax.ShapeDtypeStruct(key_weight.shape, jnp.bfloat16),
+        ),
+        in_specs=[vmem] * 6,
+        out_specs=(hbm, vmem, hbm, hbm),
+        scratch_shapes=[
+            pltpu.VMEM(w_query.shape, jnp.bfloat16),
+            pltpu.VMEM(key_weight.shape, jnp.bfloat16),
+            dma((1 + 2 * CHUNKS,)),
+        ],
+        compiler_params=pltpu.CompilerParams(vmem_limit_bytes=24 * 1024 * 1024),
+        cost_estimate=pl.CostEstimate(
+            flops=w_query.size + key_weight.size,
+            bytes_accessed=4 * (w_query.size + key_weight.size),
+            transcendentals=0,
+        ),
+    )(attended, q_factor, k_factor, maxima, w_query, key_weight)
 
 
 def solution(mesh):

time: 48.6 us -> 45.6 us (0.938)
  other arithmetic: 5.04 us -> 0 us
  Pallas kernels: 41.3 us -> 44.7 us
  local copies, waits for them, and re-layouts: 1.49 us -> 0.01 us
    convert_element_type x2 -> x0, other arithmetic: 5.04 us -> none  [the longest x1 3.17 us: shards(): (w_query.astype(jnp.float32) * q_factor).astype(jnp.bfloat16)]
    pallas_call x0 -> x1, Pallas kernels: none -> 3.61 us  [shards(): pl.pallas_call(functools.partial(finish_kernel, heads), name='finish', ou...]
    unnamed x5 -> x4, local copies, waits for them, and re-layouts: 0.98 us -> 0.01 us
    squeeze x1 -> x0, local copies, waits for them, and re-layouts: 0.51 us -> none  [shards(): return (attended, maxima[0, :heads], w_query_clipped, clipped_key_weight)]
where the time goes in v1:
time: 45.6 us; the launch traced here: 45.4 us
  Pallas kernels  44.7 us (98%)
  between operations  0.67 us (1%)
    pallas_call x1, Pallas kernels, shards(): pl.pallas_call(functools.partial(attend_kernel, n, tp_n, heads, kv_heads,...  41.1 us
    pallas_call x1, Pallas kernels, shards(): pl.pallas_call(functools.partial(finish_kernel, heads), name='finish', ou...  3.61 us

profile of v1, /device:TPU:0, one launch (start us, length us, event | category | flops | bytes accessed | tf_op | source)
XLA Modules:
  0.0 45.4 jit_solution(7443124084594017523)
XLA Ops:
  0.6 0.0 copy-start.1
  0.6 0.0 copy-start
  0.7 41.1 %attend.1 = (bf16[256,2048]{1,0:T(8,128)(2,1)S(1)}, f32[1,2048]{1,0:T(1,128)S(1)}, f32[1,1024]{1,0:T(1,128)S(1)}, f32[1,128]{1,0:T(1,128)S(1)}) custom-call(bf16[256,2048]{1,0:T(8,128)(2,1)} %q_hbm.1, bf16[256,256]{1,0:T(8,128)(2,1)} %k_hbm.1, bf16[256,256]{1,0:T(8,128)(2,1)} %v_hbm.1), custom_call_target="tpu_custom_call" | custom-call | flops 4294967296 | bytes 2097152 | tf_op jit(solution)/shard_map/attend/pallas_call | solution.py:278
  41.8 0.0 copy-done.1
  41.8 0.0 copy-done
  41.8 3.6 %finish.1 = (bf16[256,2048]{1,0:T(8,128)(2,1)}, f32[16]{0:T(128)}, bf16[1024,2048]{1,0:T(8,128)(2,1)}, bf16[1024,1024]{1,0:T(8,128)(2,1)}) custom-call(bf16[256,2048]{1,0:T(8,128)(2,1)S(1)} %get-tuple-element.8.a_ref, f32[1,2048]{1,0:T(1,128)S(1)} %get-tuple-element.9.qf_ref, f32[1,1024]{1,0:T(1,128)S(1)} %get-tuple-element.10.kf_ref, ...), custom_call_target="tpu_custom_call" | custom-call | flops 3145728 | bytes 12582912 | tf_op jit(solution)/shard_map/finish/pallas_call | solution.py:321
Async XLA Ops:
  0.6 41.2 %copy-start.1 = (bf16[1024,1024]{1,0:T(8,128)(2,1)S(1)}, bf16[1024,1024]{1,0:T(8,128)(2,1)}, u32[]{:S(2)}) copy-start(bf16[1024,1024]{1,0:T(8,128)(2,1)} %kw_ref.1) | copy-start | bytes 6291460
  0.6 41.2 %copy-start = (bf16[1024,2048]{1,0:T(8,128)(2,1)S(1)}, bf16[1024,2048]{1,0:T(8,128)(2,1)}, u32[]{:S(2)}) copy-start(bf16[1024,2048]{1,0:T(8,128)(2,1)} %w_ref.1) | copy-start | bytes 12582916

commit v2 on v1

v2 whole, which is shorter than its diff:
```python
import functools
import math

import jax
import jax.numpy as jnp
from jax import lax
from jax.experimental import pallas as pl
from jax.experimental.pallas import tpu as pltpu
from jax.sharding import PartitionSpec as P

HEAD_SIZE = 128
LANES = 128

clip_threshold = 10.0
WINDOW = 7
UP, RIGHT, LEFT = range(3)
MESH = pl.DeviceIdType.MESH


def grid_of(n):
    columns = max(d for d in range(1, n + 1) if n % d == 0 and d * d <= n)
    return n // columns, columns


def attend_kernel(
    n, tp_n, heads, kv_heads, rows, slots,
    q_hbm, k_hbm, v_hbm, w_hbm, kw_hbm,
    acc, qf_ref, kf_ref, hm_ref, w_ref, kw_ref,
    qv, kv, kt, mrun, pb, kp, mxl, mxb,
    lq, lkv, lw, recv, send, mx_recv, mx_send,
):
    group = heads // kv_heads
    nz, nx = grid_of(n)
    me = lax.axis_index("seq")
    tp = lax.axis_index("tp")
    z, x = lax.div(me, nx), lax.rem(me, nx)
    everyone = n * tp_n
    mine = me * tp_n + tp
    alone = slots == n - 1

    def head_cols(h):
        return pl.ds(h * HEAD_SIZE, HEAD_SIZE)

    def peer(d):
        other = lax.rem(mine + d, everyone)
        return {"seq": lax.div(other, tp_n), "tp": lax.rem(other, tp_n)}

    for g in range(kv_heads):
        for kind, hbm in enumerate((k_hbm, v_hbm)):
            pltpu.make_async_copy(hbm.at[:, head_cols(g)], kv.at[me, kind, g], lkv).start()
    q_copy = pltpu.make_async_copy(q_hbm, qv, lq)
    q_copy.start()

    barrier = pltpu.get_barrier_semaphore()

    @pl.loop(1, everyone)
    def _(d):
        pl.semaphore_signal(barrier, inc=1, device_id=peer(d), device_id_type=MESH)

    pltpu.make_async_copy(kv.at[me], kv.at[me], lkv).wait()
    pl.semaphore_wait(barrier, everyone - 1)

    def piece(kind, block, g, way, target):
        ref = kv.at[block, kind, g]
        return pltpu.make_async_remote_copy(
            src_ref=ref, dst_ref=ref, send_sem=send.at[way, block], recv_sem=recv.at[kind, block, g],
            device_id={"seq": target}, device_id_type=MESH,
        )

    def routes(kind, row, col):
        up = col == x
        right = col <= x
        if kind == 1:
            up = up | ((row == z) & (col == x - 1))
            right = right & jnp.logical_not((row == z - 1) & (col == x))
        return (
            up & (z + 1 < nz),
            right & (x + 1 < nx),
            (col >= x) & (x > 0) & (row < z),
        )

    towards = (lax.rem(me + nx, n), lax.rem(me + 1, n), lax.rem(me + n - 1, n))

    def each_send(kind, g, row, col, ways=(UP, RIGHT, LEFT)):
        on = routes(kind, row, col)
        for way in ways:
            @pl.when(on[way])
            def _():
                piece(kind, row * nx + col, g, way, towards[way]).start()

    def await_sent(row, col):
        block = row * nx + col
        for way, (key, value) in enumerate(zip(routes(0, row, col), routes(1, row, col))):
            def done(ref):
                pltpu.make_async_remote_copy(
                    src_ref=ref, dst_ref=ref, send_sem=send.at[way, block], recv_sem=recv.at[0, block, 0],
                    device_id={"seq": towards[way]}, device_id_type=MESH,
                ).wait_send()

            @pl.when(key & value)
            def _():
                done(kv.at[block])

            @pl.when(key & jnp.logical_not(value))
            def _():
                done(kv.at[block, 0])

            @pl.when(value & jnp.logical_not(key))
            def _():
                done(kv.at[block, 1])

    for g in range(kv_heads):
        each_send(0, g, z, x, (UP, RIGHT))
    each_send(1, 0, z, x, (UP, RIGHT))

    def rest_of_own():
        for g in range(1, kv_heads):
            each_send(1, g, z, x, (UP, RIGHT))

    @pl.when(z == 0)
    def _():
        rest_of_own()

    q_copy.wait()

    scale = HEAD_SIZE ** (-0.5)
    to_exp2 = scale * math.log2(math.e)
    ones = jnp.ones((rows, LANES), jnp.bfloat16)

    def wide(a):
        return jnp.concatenate([a] * (rows // LANES), axis=1)

    def widest(s):
        top = s[:, :LANES]
        for i in range(1, rows // LANES):
            top = jnp.maximum(top, s[:, i * LANES:(i + 1) * LANES])
        return jnp.broadcast_to(jnp.max(top, axis=1, keepdims=True), (rows, LANES))

    def place(t):
        below = jnp.where(z > 0, 1, 0)
        along = t - below
        beside = (along >= 1) & (along <= x)
        u = jnp.where(t == below, 0, jnp.maximum(t - x - 1, 0))
        w = jnp.maximum(u - 1, 0)
        k = 1 + lax.div(w, nx)
        j = lax.rem(w, nx) + jnp.where(k == z, 1, 0)
        up = jnp.where(u == 0, 1, jnp.where(j == 0, k + 1, k))
        left = jnp.where(u == 0, 0, j)
        row = jnp.where(beside, z, z - up)
        col = jnp.where(beside, x - along, lax.rem(x + nx - left, nx))
        column = t <= z
        beside = (t > z) & (t <= z + x)
        v = jnp.maximum(t - z - x - 1, 0)
        inner_row = jnp.where(column, z - t, jnp.where(beside, z, z - 1 - lax.div(v, nx - 1)))
        inner_col = jnp.where(
            column, x, jnp.where(beside, x - t + z, lax.rem(x + nx - 1 - lax.rem(v, nx - 1), nx))
        )
        edge = x + 1 == nx
        return jnp.where(edge, row, inner_row), jnp.where(edge, col, inner_col)

    def take(kind, g, t):
        row, col = place(t)
        piece(kind, row * nx + col, g, RIGHT, towards[RIGHT]).wait_recv()
        each_send(kind, g, row, col)

    def own_part(g):
        kt[g] = kv[me, 0, g].T
        r = lax.broadcasted_iota(jnp.int32, (rows, rows), 0)
        c = lax.broadcasted_iota(jnp.int32, (rows, rows), 1)
        for i in range(group):
            h = g * group + i
            s = jnp.dot(qv[:, h * HEAD_SIZE:(h + 1) * HEAD_SIZE], kt[g], preferred_element_type=jnp.float32)
            s = jnp.where(r >= c, s, jnp.float32(-1e30))
            top = widest(s)
            mrun[h] = top
            p = jnp.exp2((s - wide(top)) * to_exp2).astype(jnp.bfloat16)
            v_ones = jnp.concatenate([kv[me, 1, g], ones], axis=1)
            acc[h] = jnp.dot(p, v_ones, preferred_element_type=jnp.float32)

    def score_part(g, t):
        row, col = place(t)
        kt[g] = kv[row * nx + col, 0, g].T
        slot = lax.rem(t - 1, slots)
        for i in range(group):
            h = g * group + i
            s = jnp.dot(qv[:, h * HEAD_SIZE:(h + 1) * HEAD_SIZE], kt[g], preferred_element_type=jnp.float32)
            old = mrun[h]
            top = jnp.maximum(old, widest(s))
            mrun[h] = top
            kp[slot, h] = jnp.exp2((old - top) * to_exp2)
            pb[slot, h] = jnp.exp2((s - wide(top)) * to_exp2).astype(jnp.bfloat16)

    def value_part(g, t):
        row, col = place(t)
        block = row * nx + col
        slot = lax.rem(t - 1, slots)
        for i in range(group):
            h = g * group + i
            v_ones = jnp.concatenate([kv[block, 1, g], ones], axis=1)
            keep = kp[slot, h]
            acc[h] = acc[h] * jnp.concatenate([keep, keep], axis=1) + jnp.dot(
                pb[slot, h], v_ones, preferred_element_type=jnp.float32
            )

    weight_copies = [
        pltpu.make_async_copy(w_hbm, w_ref, lw.at[0]), pltpu.make_async_copy(kw_hbm, kw_ref, lw.at[1])
    ]
    for copy in weight_copies:
        copy.start()

    for g in range(kv_heads):
        own_part(g)

    def score_step(t):
        row, col = place(t)
        for g in range(kv_heads):
            take(0, g, t)
            if g == kv_heads - 1:
                @pl.when((row == 0) & (col == x))
                def _():
                    rest_of_own()
            score_part(g, t)

    last = z + 1 == nz

    def early(t):
        column = place(t)[1] == x
        soon = jnp.where(x + 1 < nx, (t >= 2) & (t < z), t == 1)
        return column & jnp.where(last, soon, z >= 1)

    def ahead(t):
        column = place(t)[1] == x
        return last & column & (t > 2) & (t <= me) & jnp.logical_not(early(t))

    def take_values(t):
        for g in range(kv_heads):
            take(1, g, t)

    def value_step(t):
        if alone:
            @pl.when(last & jnp.logical_not(early(t) | ahead(t)))
            def _():
                take_values(t)

            @pl.when(ahead(t + 2))
            def _():
                take_values(t + 2)
        else:
            take_values(t)

        for g in range(kv_heads):
            value_part(g, t)
        @pl.when(t > 2)
        def _():
            await_sent(*place(t - 2))

    lane = lax.broadcasted_iota(jnp.int32, (1, LANES), 1)
    def mx_copy(d, owner):
        return pltpu.make_async_remote_copy(
            src_ref=mxl, dst_ref=mxb.at[owner], send_sem=mx_send,
            recv_sem=mx_recv, device_id=peer(d), device_id_type=MESH,
        )

    def send_maxima():
        local = jnp.full((1, LANES), -1e30, jnp.float32)
        for h in range(heads):
            local = jnp.where(lane == h, jnp.max(mrun[h], axis=0, keepdims=True), local)
        mxl[...] = local
        mxb[mine] = local

        @pl.loop(1, everyone)
        def _(d):
            mx_copy(d, mine).start()

    if alone:
        @pl.loop(1, me + 1)
        def _(t):
            @pl.when(t == me)
            def _():
                @pl.loop(1, me + 1)
                def _(s):
                    @pl.when(early(s))
                    def _():
                        take_values(s)

            score_step(t)

        send_maxima()

        @pl.loop(1, jnp.where(last, 1, me + 1))
        def _(t):
            @pl.when(jnp.logical_not(early(t)))
            def _():
                take_values(t)

        @pl.loop(1, me + 1)
        def _(t):
            value_step(t)
    else:
        @pl.loop(1, me + 1)
        def _(t):
            score_step(t)
            value_step(t)

        send_maxima()

    others = mxb.at[pl.ds(0, everyone - 1)]
    exchange = pltpu.make_async_remote_copy(
        src_ref=others, dst_ref=others, send_sem=mx_send, recv_sem=mx_recv,
        device_id=peer(1), device_id_type=MESH,
    )
    exchange.wait_recv()

    def widest_lanes(a, keep):
        return jnp.broadcast_to(
            jnp.max(jnp.where(keep, a, -1e30), axis=1, keepdims=True), (1, LANES)
        )

    def clip_of(top):
        return clip_threshold / jnp.maximum(top * scale, clip_threshold)

    def shard_top(owner):
        top = mxb[owner]
        for i in range(1, n):
            top = jnp.maximum(top, mxb[i * tp_n + owner])
        return top

    def in_group(g):
        return (lane >= g * group) & (lane < (g + 1) * group)

    top = shard_top(tp)
    hm_ref[...] = top * scale
    clip = [clip_of(widest_lanes(top, in_group(g))) for g in range(kv_heads)]
    for h in range(heads):
        qf_ref[:, h * HEAD_SIZE:(h + 1) * HEAD_SIZE] = clip_of(
            widest_lanes(top, lane == h)
        ) / jnp.sqrt(clip[h // group])
    for owner in range(tp_n):
        other = shard_top(owner)
        for g in range(kv_heads):
            at = (owner * kv_heads + g) * HEAD_SIZE
            kf_ref[:, at:at + HEAD_SIZE] = jnp.sqrt(clip_of(widest_lanes(other, in_group(g))))

    await_sent(z, x)

    @pl.loop(jnp.maximum(me - 1, 1), me + 1)
    def _(t):
        await_sent(*place(t))

    for copy in weight_copies:
        copy.wait()

    exchange.wait_send()


CHUNKS = 8


def finish_kernel(heads, acc, qf_ref, kf_ref, hm_ref, w_ref, kw_ref, a_hbm, top_ref, w_hbm, kw_hbm, wb, kwb, ab, sem):
    for at, src, factor, buf, dst in ((0, w_ref, qf_ref, wb, w_hbm), (1, kw_ref, kf_ref, kwb, kw_hbm)):
        size = src.shape[0] // CHUNKS
        for i in range(CHUNKS):
            rows = pl.ds(i * size, size)
            buf[rows, :] = (src[rows, :].astype(jnp.float32) * factor[...]).astype(jnp.bfloat16)
            pltpu.make_async_copy(buf.at[rows], dst.at[rows], sem.at[at]).start()
    top_ref[...] = hm_ref[0, :heads]
    for h in range(heads):
        cols = slice(h * HEAD_SIZE, (h + 1) * HEAD_SIZE)
        a = acc[h]
        ab[:, cols] = (a[:, :HEAD_SIZE] / a[:, HEAD_SIZE:]).astype(jnp.bfloat16)
        pltpu.make_async_copy(ab.at[:, cols], a_hbm.at[:, cols], sem.at[2]).start()
    for at, buf, dst in ((0, wb, w_hbm), (1, kwb, kw_hbm), (2, ab, a_hbm)):
        pltpu.make_async_copy(buf, dst, sem.at[at]).wait()


def shards(n, tp_n, queries, keys, values, w_query, key_weight):
    rows = queries.shape[0]
    heads = queries.shape[1] // HEAD_SIZE
    kv_heads = keys.shape[1] // HEAD_SIZE
    slots = n - 1 if n - 1 <= WINDOW else 1
    everyone = n * tp_n
    vmem = pl.BlockSpec(memory_space=pltpu.VMEM)
    hbm = pl.BlockSpec(memory_space=pltpu.HBM)
    dma = pltpu.SemaphoreType.DMA
    acc, q_factor, k_factor, maxima, w_local, kw_local = pl.pallas_call(
        functools.partial(attend_kernel, n, tp_n, heads, kv_heads, rows, slots),
        name="attend",
        out_shape=(
            jax.ShapeDtypeStruct((heads, rows, 2 * HEAD_SIZE), jnp.float32),
            jax.ShapeDtypeStruct((1, heads * HEAD_SIZE), jnp.float32),
            jax.ShapeDtypeStruct((1, key_weight.shape[1]), jnp.float32),
            jax.ShapeDtypeStruct((1, LANES), jnp.float32),
            jax.ShapeDtypeStruct(w_query.shape, jnp.bfloat16),
            jax.ShapeDtypeStruct(key_weight.shape, jnp.bfloat16),
        ),
        in_specs=[hbm] * 5,
        out_specs=[vmem] * 6,
        scratch_shapes=[
            pltpu.VMEM((rows, heads * HEAD_SIZE), jnp.bfloat16),
            pltpu.VMEM((n, 2, kv_heads, rows, HEAD_SIZE), jnp.bfloat16),
            pltpu.VMEM((kv_heads, HEAD_SIZE, rows), jnp.bfloat16),
            pltpu.VMEM((heads, rows, LANES), jnp.float32),
            pltpu.VMEM((slots, heads, rows, rows), jnp.bfloat16),
            pltpu.VMEM((slots, heads, rows, LANES), jnp.float32),
            pltpu.VMEM((1, LANES), jnp.float32),
            pltpu.VMEM((everyone, 1, LANES), jnp.float32),
            dma,
            dma,
            dma((2,)),
            dma((2, n, kv_heads)),
            dma((3, n)),
            dma,
            dma,
        ],
        compiler_params=pltpu.CompilerParams(
            collective_id=0, has_side_effects=True, vmem_limit_bytes=36 * 1024 * 1024
        ),
        cost_estimate=pl.CostEstimate(
            flops=4 * rows * rows * n * heads * HEAD_SIZE,
            bytes_accessed=4 * rows * heads * HEAD_SIZE,
            transcendentals=rows * rows * n * heads,
        ),
    )(*(
        pltpu.with_memory_space_constraint(a, pltpu.HBM)
        for a in (queries, keys, values, w_query, key_weight)
    ))
    return pl.pallas_call(
        functools.partial(finish_kernel, heads),
        name="finish",
        out_shape=(
            jax.ShapeDtypeStruct(queries.shape, jnp.bfloat16),
            jax.ShapeDtypeStruct((heads,), jnp.float32),
            jax.ShapeDtypeStruct(w_query.shape, jnp.bfloat16),
            jax.ShapeDtypeStruct(key_weight.shape, jnp.bfloat16),
        ),
        in_specs=[vmem] * 6,
        out_specs=(hbm, vmem, hbm, hbm),
        scratch_shapes=[
            pltpu.VMEM(w_query.shape, jnp.bfloat16),
            pltpu.VMEM(key_weight.shape, jnp.bfloat16),
            pltpu.VMEM(queries.shape, jnp.bfloat16),
            dma((3,)),
        ],
        compiler_params=pltpu.CompilerParams(vmem_limit_bytes=24 * 1024 * 1024),
        cost_estimate=pl.CostEstimate(
            flops=w_query.size + key_weight.size,
            bytes_accessed=4 * (w_query.size + key_weight.size),
            transcendentals=0,
        ),
    )(acc, q_factor, k_factor, maxima, w_local, kw_local)


def solution(mesh):
    in_specs = (P("seq", "tp"), P("seq", "tp"), P("seq", "tp"), P("seq", "tp"), P("seq", None))
    out_specs = (P("seq", "tp"), P("tp"), P("seq", "tp"), P("seq", None))
    body = functools.partial(shards, mesh.shape["seq"], mesh.shape["tp"])
    return jax.shard_map(body, mesh=mesh, in_specs=in_specs, out_specs=out_specs, check_vma=False)
```

time: 45.6 us -> 34.9 us (0.77)
  Pallas kernels: 44.7 us -> 34.1 us
    pallas_call x1, Pallas kernels: 41.1 us -> 30.6 us  [shards(): pl.pallas_call(functools.partial(attend_kernel, n, tp_n, heads, kv_heads,...]
where the time goes in v2:
time: 34.9 us; the launch traced here: 34.8 us
  Pallas kernels  34.1 us (98%)
  between operations  0.64 us (2%)
    pallas_call x1, Pallas kernels, shards(): pl.pallas_call(functools.partial(attend_kernel, n, tp_n, heads, kv_heads,...  30.6 us
    pallas_call x1, Pallas kernels, shards(): pl.pallas_call(functools.partial(finish_kernel, heads), name='finish', ou...  3.55 us

profile of v2, /device:TPU:0, one launch (start us, length us, event | category | flops | bytes accessed | tf_op | source)
XLA Modules:
  0.0 34.8 jit_solution(9191832814496437554)
XLA Ops:
  0.6 30.6 %attend.1 = (f32[16,256,256]{2,1,0:T(8,128)S(1)}, f32[1,2048]{1,0:T(1,128)S(1)}, f32[1,1024]{1,0:T(1,128)S(1)}, f32[1,128]{1,0:T(1,128)S(1)}, bf16[1024,2048]{1,...) custom-call(bf16[256,2048]{1,0:T(8,128)(2,1)} %q_hbm.1, bf16[256,256]{1,0:T(8,128)(2,1)} %k_hbm.1, bf16[256,256]{1,0:T(8,128)(2,1)} %v_hbm.1, ...), custom_call_target="tpu_custom_call" | custom-call | flops 4294967296 | bytes 2097152 | tf_op jit(solution)/shard_map/attend/pallas_call | solution.py:385
  31.2 3.6 %finish.1 = (bf16[256,2048]{1,0:T(8,128)(2,1)}, f32[16]{0:T(128)}, bf16[1024,2048]{1,0:T(8,128)(2,1)}, bf16[1024,1024]{1,0:T(8,128)(2,1)}) custom-call(f32[16,256,256]{2,1,0:T(8,128)S(1)} %get-tuple-element.10.acc, f32[1,2048]{1,0:T(1,128)S(1)} %get-tuple-element.11.qf_ref, f32[1,1024]{1,0:T(1,128)S(1)} %get-tuple-element.12.kf_ref, ...), custom_call_target="tpu_custom_call" | custom-call | flops 3145728 | bytes 12582912 | tf_op jit(solution)/shard_map/finish/pallas_call | solution.py:427

commit v3 on v2

--- a/solution.py
+++ b/solution.py
@@ -10,6 +10,7 @@
 
 HEAD_SIZE = 128
 LANES = 128
+SUMS = 16
 
 clip_threshold = 10.0
 WINDOW = 7
@@ -26,7 +27,7 @@
     n, tp_n, heads, kv_heads, rows, slots,
     q_hbm, k_hbm, v_hbm, w_hbm, kw_hbm,
     acc, qf_ref, kf_ref, hm_ref, w_ref, kw_ref,
-    qv, kv, kt, mrun, pb, kp, mxl, mxb,
+    qv, kv, qt, vt, mrun, pb, kp, mxl, mxb,
     lq, lkv, lw, recv, send, mx_recv, mx_send,
 ):
     group = heads // kv_heads
@@ -125,16 +126,6 @@
 
     scale = HEAD_SIZE ** (-0.5)
     to_exp2 = scale * math.log2(math.e)
-    ones = jnp.ones((rows, LANES), jnp.bfloat16)
-
-    def wide(a):
-        return jnp.concatenate([a] * (rows // LANES), axis=1)
-
-    def widest(s):
-        top = s[:, :LANES]
-        for i in range(1, rows // LANES):
-            top = jnp.maximum(top, s[:, i * LANES:(i + 1) * LANES])
-        return jnp.broadcast_to(jnp.max(top, axis=1, keepdims=True), (rows, LANES))
 
     def place(t):
         below = jnp.where(z > 0, 1, 0)
@@ -148,15 +139,7 @@
         left = jnp.where(u == 0, 0, j)
         row = jnp.where(beside, z, z - up)
         col = jnp.where(beside, x - along, lax.rem(x + nx - left, nx))
-        column = t <= z
-        beside = (t > z) & (t <= z + x)
-        v = jnp.maximum(t - z - x - 1, 0)
-        inner_row = jnp.where(column, z - t, jnp.where(beside, z, z - 1 - lax.div(v, nx - 1)))
-        inner_col = jnp.where(
-            column, x, jnp.where(beside, x - t + z, lax.rem(x + nx - 1 - lax.rem(v, nx - 1), nx))
-        )
-        edge = x + 1 == nx
-        return jnp.where(edge, row, inner_row), jnp.where(edge, col, inner_col)
+        return row, col
 
     def take(kind, g, t):
         row, col = place(t)
@@ -164,43 +147,48 @@
         each_send(kind, g, row, col)
 
     def own_part(g):
-        kt[g] = kv[me, 0, g].T
+        vt[g, :HEAD_SIZE] = kv[me, 1, g].T
         r = lax.broadcasted_iota(jnp.int32, (rows, rows), 0)
         c = lax.broadcasted_iota(jnp.int32, (rows, rows), 1)
         for i in range(group):
             h = g * group + i
-            s = jnp.dot(qv[:, h * HEAD_SIZE:(h + 1) * HEAD_SIZE], kt[g], preferred_element_type=jnp.float32)
-            s = jnp.where(r >= c, s, jnp.float32(-1e30))
-            top = widest(s)
+            s = lax.dot_general(
+                kv[me, 0, g], qv[:, h * HEAD_SIZE:(h + 1) * HEAD_SIZE], (((1,), (1,)), ((), ())),
+                preferred_element_type=jnp.float32,
+            )
+            s = jnp.where(c >= r, s, jnp.float32(-1e30))
+            top = jnp.max(s, axis=0, keepdims=True)
             mrun[h] = top
-            p = jnp.exp2((s - wide(top)) * to_exp2).astype(jnp.bfloat16)
-            v_ones = jnp.concatenate([kv[me, 1, g], ones], axis=1)
-            acc[h] = jnp.dot(p, v_ones, preferred_element_type=jnp.float32)
-
-    def score_part(g, t):
-        row, col = place(t)
-        kt[g] = kv[row * nx + col, 0, g].T
-        slot = lax.rem(t - 1, slots)
+            pb[0, h] = jnp.exp2((s - top) * to_exp2).astype(jnp.bfloat16)
         for i in range(group):
             h = g * group + i
-            s = jnp.dot(qv[:, h * HEAD_SIZE:(h + 1) * HEAD_SIZE], kt[g], preferred_element_type=jnp.float32)
-            old = mrun[h]
-            top = jnp.maximum(old, widest(s))
-            mrun[h] = top
-            kp[slot, h] = jnp.exp2((old - top) * to_exp2)
-            pb[slot, h] = jnp.exp2((s - wide(top)) * to_exp2).astype(jnp.bfloat16)
-
-    def value_part(g, t):
+            acc[h] = jnp.dot(vt[g], pb[0, h], preferred_element_type=jnp.float32)
+
+    def score_part(g, t):
         row, col = place(t)
         block = row * nx + col
         slot = lax.rem(t - 1, slots)
         for i in range(group):
             h = g * group + i
-            v_ones = jnp.concatenate([kv[block, 1, g], ones], axis=1)
-            keep = kp[slot, h]
-            acc[h] = acc[h] * jnp.concatenate([keep, keep], axis=1) + jnp.dot(
-                pb[slot, h], v_ones, preferred_element_type=jnp.float32
+            s = jnp.dot(kv[block, 0, g], qt[h], preferred_element_type=jnp.float32)
+            old = mrun[h]
+            top = jnp.maximum(old, jnp.max(s, axis=0, keepdims=True))
+            mrun[h] = top
+            kp[slot, h] = jnp.exp2((old - top) * to_exp2)
+            pb[slot, h] = jnp.exp2((s - top) * to_exp2).astype(jnp.bfloat16)
+
+    def value_part(g, t):
+        row, col = place(t)
+        slot = lax.rem(t - 1, slots)
+        vt[g, :HEAD_SIZE] = kv[row * nx + col, 1, g].T
+        for i in range(group):
+            h = g * group + i
+            acc[h] = acc[h] * kp[slot, h] + jnp.dot(
+                vt[g], pb[slot, h], preferred_element_type=jnp.float32
             )
+
+    for g in range(kv_heads):
+        vt[g, HEAD_SIZE:] = jnp.ones((SUMS, rows), jnp.bfloat16)
 
     weight_copies = [
         pltpu.make_async_copy(w_hbm, w_ref, lw.at[0]), pltpu.make_async_copy(kw_hbm, kw_ref, lw.at[1])
@@ -210,6 +198,8 @@
 
     for g in range(kv_heads):
         own_part(g)
+    for h in range(heads):
+        qt[h] = qv[:, h * HEAD_SIZE:(h + 1) * HEAD_SIZE].T
 
     def score_step(t):
         row, col = place(t)
@@ -225,12 +215,11 @@
 
     def early(t):
         column = place(t)[1] == x
-        soon = jnp.where(x + 1 < nx, (t >= 2) & (t < z), t == 1)
-        return column & jnp.where(last, soon, z >= 1)
+        return column & jnp.where(last, (x + 1 == nx) & (t == 1), z >= 1)
 
     def ahead(t):
         column = place(t)[1] == x
-        return last & column & (t > 2) & (t <= me) & jnp.logical_not(early(t))
+        return last & column & (t > 1) & (t <= me)
 
     def take_values(t):
         for g in range(kv_heads):
@@ -241,6 +230,10 @@
             @pl.when(last & jnp.logical_not(early(t) | ahead(t)))
             def _():
                 take_values(t)
+
+            @pl.when((t == 1) & ahead(2))
+            def _():
+                take_values(2)
 
             @pl.when(ahead(t + 2))
             def _():
@@ -264,7 +257,7 @@
     def send_maxima():
         local = jnp.full((1, LANES), -1e30, jnp.float32)
         for h in range(heads):
-            local = jnp.where(lane == h, jnp.max(mrun[h], axis=0, keepdims=True), local)
+            local = jnp.where(lane == h, jnp.max(mrun[h], axis=1, keepdims=True), local)
         mxl[...] = local
         mxb[mine] = local
 
@@ -367,7 +360,7 @@
     for h in range(heads):
         cols = slice(h * HEAD_SIZE, (h + 1) * HEAD_SIZE)
         a = acc[h]
-        ab[:, cols] = (a[:, :HEAD_SIZE] / a[:, HEAD_SIZE:]).astype(jnp.bfloat16)
+        ab[:, cols] = (a[:HEAD_SIZE] / a[HEAD_SIZE:HEAD_SIZE + 1]).astype(jnp.bfloat16).T
         pltpu.make_async_copy(ab.at[:, cols], a_hbm.at[:, cols], sem.at[2]).start()
     for at, buf, dst in ((0, wb, w_hbm), (1, kwb, kw_hbm), (2, ab, a_hbm)):
         pltpu.make_async_copy(buf, dst, sem.at[at]).wait()
@@ -386,7 +379,7 @@
         functools.partial(attend_kernel, n, tp_n, heads, kv_heads, rows, slots),
         name="attend",
         out_shape=(
-            jax.ShapeDtypeStruct((heads, rows, 2 * HEAD_SIZE), jnp.float32),
+            jax.ShapeDtypeStruct((heads, HEAD_SIZE + SUMS, rows), jnp.float32),
             jax.ShapeDtypeStruct((1, heads * HEAD_SIZE), jnp.float32),
             jax.ShapeDtypeStruct((1, key_weight.shape[1]), jnp.float32),
             jax.ShapeDtypeStruct((1, LANES), jnp.float32),
@@ -398,10 +391,11 @@
         scratch_shapes=[
             pltpu.VMEM((rows, heads * HEAD_SIZE), jnp.bfloat16),
             pltpu.VMEM((n, 2, kv_heads, rows, HEAD_SIZE), jnp.bfloat16),
-            pltpu.VMEM((kv_heads, HEAD_SIZE, rows), jnp.bfloat16),
-            pltpu.VMEM((heads, rows, LANES), jnp.float32),
+            pltpu.VMEM((heads, HEAD_SIZE, rows), jnp.bfloat16),
+            pltpu.VMEM((kv_heads, HEAD_SIZE + SUMS, rows), jnp.bfloat16),
+            pltpu.VMEM((heads, 1, rows), jnp.float32),
             pltpu.VMEM((slots, heads, rows, rows), jnp.bfloat16),
-            pltpu.VMEM((slots, heads, rows, LANES), jnp.float32),
+            pltpu.VMEM((slots, heads, 1, rows), jnp.float32),
             pltpu.VMEM((1, LANES), jnp.float32),
             pltpu.VMEM((everyone, 1, LANES), jnp.float32),
             dma,
@@ -413,7 +407,7 @@
             dma,
         ],
         compiler_params=pltpu.CompilerParams(
-            collective_id=0, has_side_effects=True, vmem_limit_bytes=36 * 1024 * 1024
+            collective_id=0, has_side_effects=True, vmem_limit_bytes=30 * 1024 * 1024
         ),
         cost_estimate=pl.CostEstimate(
             flops=4 * rows * rows * n * heads * HEAD_SIZE,

time: 34.9 us -> 34 us (0.974); the launches traced: 34.8 us -> 33.5 us
  Pallas kernels: 34.1 us -> 32.8 us
    pallas_call x1, Pallas kernels: 30.6 us -> 29.2 us  [shards(): pl.pallas_call(functools.partial(attend_kernel, n, tp_n, heads, kv_heads,...]
where the time goes in v3:
time: 34 us; the launch traced here: 33.5 us
  Pallas kernels  32.8 us (96%)
  between operations  0.64 us (2%)
    pallas_call x1, Pallas kernels, shards(): pl.pallas_call(functools.partial(attend_kernel, n, tp_n, heads, kv_heads,...  29.2 us
    pallas_call x1, Pallas kernels, shards(): pl.pallas_call(functools.partial(finish_kernel, heads), name='finish', ou...  3.68 us

profile of v3, /device:TPU:0, one launch (start us, length us, event | category | flops | bytes accessed | tf_op | source)
XLA Modules:
  0.0 33.5 jit_solution(13584412185261630463)
XLA Ops:
  0.6 29.2 %attend.1 = (f32[16,144,256]{2,1,0:T(8,128)S(1)}, f32[1,2048]{1,0:T(1,128)S(1)}, f32[1,1024]{1,0:T(1,128)S(1)}, f32[1,128]{1,0:T(1,128)S(1)}, bf16[1024,2048]{1,...) custom-call(bf16[256,2048]{1,0:T(8,128)(2,1)} %q_hbm.1, bf16[256,256]{1,0:T(8,128)(2,1)} %k_hbm.1, bf16[256,256]{1,0:T(8,128)(2,1)} %v_hbm.1, ...), custom_call_target="tpu_custom_call" | custom-call | flops 4294967296 | bytes 2097152 | tf_op jit(solution)/shard_map/attend/pallas_call | solution.py:378
  29.8 3.7 %finish.1 = (bf16[256,2048]{1,0:T(8,128)(2,1)}, f32[16]{0:T(128)}, bf16[1024,2048]{1,0:T(8,128)(2,1)}, bf16[1024,1024]{1,0:T(8,128)(2,1)}) custom-call(f32[16,144,256]{2,1,0:T(8,128)S(1)} %get-tuple-element.10.acc, f32[1,2048]{1,0:T(1,128)S(1)} %get-tuple-element.11.qf_ref, f32[1,1024]{1,0:T(1,128)S(1)} %get-tuple-element.12.kf_ref, ...), custom_call_target="tpu_custom_call" | custom-call | flops 3145728 | bytes 12582912 | tf_op jit(solution)/shard_map/finish/pallas_call | solution.py:421

commit v4 on v3

--- a/solution.py
+++ b/solution.py
@@ -11,6 +11,7 @@
 HEAD_SIZE = 128
 LANES = 128
 SUMS = 16
+PARTS = 2
 
 clip_threshold = 10.0
 WINDOW = 7
@@ -61,10 +62,13 @@
     pltpu.make_async_copy(kv.at[me], kv.at[me], lkv).wait()
     pl.semaphore_wait(barrier, everyone - 1)
 
-    def piece(kind, block, g, way, target):
-        ref = kv.at[block, kind, g]
+    part_rows = rows // PARTS
+
+    def piece(kind, block, g, part, way, target):
+        ref = kv.at[block, kind, g, pl.ds(part * part_rows, part_rows)]
         return pltpu.make_async_remote_copy(
-            src_ref=ref, dst_ref=ref, send_sem=send.at[way, block], recv_sem=recv.at[kind, block, g],
+            src_ref=ref, dst_ref=ref, send_sem=send.at[way, block],
+            recv_sem=recv.at[kind, block, g, part],
             device_id={"seq": target}, device_id_type=MESH,
         )
 
@@ -82,19 +86,20 @@
 
     towards = (lax.rem(me + nx, n), lax.rem(me + 1, n), lax.rem(me + n - 1, n))
 
-    def each_send(kind, g, row, col, ways=(UP, RIGHT, LEFT)):
+    def each_send(kind, g, row, col, ways=(UP, RIGHT, LEFT), parts=range(PARTS)):
         on = routes(kind, row, col)
         for way in ways:
             @pl.when(on[way])
             def _():
-                piece(kind, row * nx + col, g, way, towards[way]).start()
+                for part in parts:
+                    piece(kind, row * nx + col, g, part, way, towards[way]).start()
 
     def await_sent(row, col):
         block = row * nx + col
         for way, (key, value) in enumerate(zip(routes(0, row, col), routes(1, row, col))):
             def done(ref):
                 pltpu.make_async_remote_copy(
-                    src_ref=ref, dst_ref=ref, send_sem=send.at[way, block], recv_sem=recv.at[0, block, 0],
+                    src_ref=ref, dst_ref=ref, send_sem=send.at[way, block], recv_sem=recv.at[0, block, 0, 0],
                     device_id={"seq": towards[way]}, device_id_type=MESH,
                 ).wait_send()
 
@@ -143,8 +148,9 @@
 
     def take(kind, g, t):
         row, col = place(t)
-        piece(kind, row * nx + col, g, RIGHT, towards[RIGHT]).wait_recv()
-        each_send(kind, g, row, col)
+        for part in range(PARTS):
+            piece(kind, row * nx + col, g, part, RIGHT, towards[RIGHT]).wait_recv()
+            each_send(kind, g, row, col, parts=(part,))
 
     def own_part(g):
         vt[g, :HEAD_SIZE] = kv[me, 1, g].T
@@ -227,15 +233,11 @@
 
     def value_step(t):
         if alone:
-            @pl.when(last & jnp.logical_not(early(t) | ahead(t)))
+            @pl.when(last & (t > 1) & jnp.logical_not(ahead(t)))
             def _():
                 take_values(t)
 
-            @pl.when((t == 1) & ahead(2))
-            def _():
-                take_values(2)
-
-            @pl.when(ahead(t + 2))
+            @pl.when((t > 1) & ahead(t + 2))
             def _():
                 take_values(t + 2)
         else:
@@ -277,6 +279,17 @@
                         take_values(s)
 
             score_step(t)
+
+        @pl.when(last & (me > 0))
+        def _():
+            @pl.when(jnp.logical_not(early(1)))
+            def _():
+                take_values(1)
+
+            for t in (2, 3):
+                @pl.when(ahead(t))
+                def _():
+                    take_values(t)
 
         send_maxima()
 
@@ -401,7 +414,7 @@
             dma,
             dma,
             dma((2,)),
-            dma((2, n, kv_heads)),
+            dma((2, n, kv_heads, PARTS)),
             dma((3, n)),
             dma,
             dma,

time: 34 us -> 33.4 us (0.982)
  Pallas kernels: 32.8 us -> 32.3 us
    pallas_call x1, Pallas kernels: 29.2 us -> 28.6 us  [shards(): pl.pallas_call(functools.partial(attend_kernel, n, tp_n, heads, kv_heads,...]
where the time goes in v4:
time: 33.4 us; the launch traced here: 33 us
  Pallas kernels  32.3 us (97%)
  between operations  0.64 us (2%)
    pallas_call x1, Pallas kernels, shards(): pl.pallas_call(functools.partial(attend_kernel, n, tp_n, heads, kv_heads,...  28.6 us
    pallas_call x1, Pallas kernels, shards(): pl.pallas_call(functools.partial(finish_kernel, heads), name='finish', ou...  3.68 us

profile of v4, /device:TPU:0, one launch (start us, length us, event | category | flops | bytes accessed | tf_op | source)
XLA Modules:
  0.0 33.0 jit_solution(17669729939206504419)
XLA Ops:
  0.6 28.6 %attend.1 = (f32[16,144,256]{2,1,0:T(8,128)S(1)}, f32[1,2048]{1,0:T(1,128)S(1)}, f32[1,1024]{1,0:T(1,128)S(1)}, f32[1,128]{1,0:T(1,128)S(1)}, bf16[1024,2048]{1,...) custom-call(bf16[256,2048]{1,0:T(8,128)(2,1)} %q_hbm.1, bf16[256,256]{1,0:T(8,128)(2,1)} %k_hbm.1, bf16[256,256]{1,0:T(8,128)(2,1)} %v_hbm.1, ...), custom_call_target="tpu_custom_call" | custom-call | flops 4294967296 | bytes 2097152 | tf_op jit(solution)/shard_map/attend/pallas_call | solution.py:391
  29.3 3.7 %finish.1 = (bf16[256,2048]{1,0:T(8,128)(2,1)}, f32[16]{0:T(128)}, bf16[1024,2048]{1,0:T(8,128)(2,1)}, bf16[1024,1024]{1,0:T(8,128)(2,1)}) custom-call(f32[16,144,256]{2,1,0:T(8,128)S(1)} %get-tuple-element.10.acc, f32[1,2048]{1,0:T(1,128)S(1)} %get-tuple-element.11.qf_ref, f32[1,1024]{1,0:T(1,128)S(1)} %get-tuple-element.12.kf_ref, ...), custom_call_target="tpu_custom_call" | custom-call | flops 3145728 | bytes 12582912 | tf_op jit(solution)/shard_map/finish/pallas_call | solution.py:434

commit v5 on v4

--- a/solution.py
+++ b/solution.py
@@ -43,9 +43,19 @@
     def head_cols(h):
         return pl.ds(h * HEAD_SIZE, HEAD_SIZE)
 
-    def peer(d):
-        other = lax.rem(mine + d, everyone)
-        return {"seq": lax.div(other, tp_n), "tp": lax.rem(other, tp_n)}
+    columns = [lax.rem(tp + e, tp_n) for e in range(tp_n)]
+
+    def each_peer(act):
+        @pl.loop(0, n)
+        def _(d):
+            row = lax.rem(me + d, n)
+
+            @pl.when(d > 0)
+            def _():
+                act({"seq": row, "tp": tp})
+
+            for e in range(1, tp_n):
+                act({"seq": row, "tp": columns[e]})
 
     for g in range(kv_heads):
         for kind, hbm in enumerate((k_hbm, v_hbm)):
@@ -55,9 +65,7 @@
 
     barrier = pltpu.get_barrier_semaphore()
 
-    @pl.loop(1, everyone)
-    def _(d):
-        pl.semaphore_signal(barrier, inc=1, device_id=peer(d), device_id_type=MESH)
+    each_peer(lambda peer: pl.semaphore_signal(barrier, inc=1, device_id=peer, device_id_type=MESH))
 
     pltpu.make_async_copy(kv.at[me], kv.at[me], lkv).wait()
     pl.semaphore_wait(barrier, everyone - 1)
@@ -250,10 +258,10 @@
             await_sent(*place(t - 2))
 
     lane = lax.broadcasted_iota(jnp.int32, (1, LANES), 1)
-    def mx_copy(d, owner):
+    def mx_copy(peer):
         return pltpu.make_async_remote_copy(
-            src_ref=mxl, dst_ref=mxb.at[owner], send_sem=mx_send,
-            recv_sem=mx_recv, device_id=peer(d), device_id_type=MESH,
+            src_ref=mxl, dst_ref=mxb.at[mine], send_sem=mx_send,
+            recv_sem=mx_recv, device_id=peer, device_id_type=MESH,
         )
 
     def send_maxima():
@@ -263,9 +271,7 @@
         mxl[...] = local
         mxb[mine] = local
 
-        @pl.loop(1, everyone)
-        def _(d):
-            mx_copy(d, mine).start()
+        each_peer(lambda peer: mx_copy(peer).start())
 
     if alone:
         @pl.loop(1, me + 1)
@@ -313,7 +319,7 @@
     others = mxb.at[pl.ds(0, everyone - 1)]
     exchange = pltpu.make_async_remote_copy(
         src_ref=others, dst_ref=others, send_sem=mx_send, recv_sem=mx_recv,
-        device_id=peer(1), device_id_type=MESH,
+        device_id={"seq": towards[RIGHT]}, device_id_type=MESH,
     )
     exchange.wait_recv()
 
@@ -414,8 +420,8 @@
             dma,
             dma,
             dma((2,)),
-            dma((2, n, kv_heads, PARTS)),
-            dma((3, n)),
+            dma((2, n - 1, kv_heads, PARTS)),
+            dma((3, n - 1)),
             dma,
             dma,
         ],

time: 33.4 us -> 33.2 us (level)
  no operation moved by 1% of the time
where the time goes in v5:
time: 33.2 us; the launch traced here: 32.8 us
  Pallas kernels  32.2 us (97%)
  between operations  0.64 us (2%)
    pallas_call x1, Pallas kernels, shards(): pl.pallas_call(functools.partial(attend_kernel, n, tp_n, heads, kv_heads,...  28.5 us
    pallas_call x1, Pallas kernels, shards(): pl.pallas_call(functools.partial(finish_kernel, heads), name='finish', ou...  3.68 us

profile of v5, /device:TPU:0, one launch (start us, length us, event | category | flops | bytes accessed | tf_op | source)
XLA Modules:
  0.0 32.8 jit_solution(11743626154716157365)
XLA Ops:
  0.6 28.5 %attend.1 = (f32[16,144,256]{2,1,0:T(8,128)S(1)}, f32[1,2048]{1,0:T(1,128)S(1)}, f32[1,1024]{1,0:T(1,128)S(1)}, f32[1,128]{1,0:T(1,128)S(1)}, bf16[1024,2048]{1,...) custom-call(bf16[256,2048]{1,0:T(8,128)(2,1)} %q_hbm.1, bf16[256,256]{1,0:T(8,128)(2,1)} %k_hbm.1, bf16[256,256]{1,0:T(8,128)(2,1)} %v_hbm.1, ...), custom_call_target="tpu_custom_call" | custom-call | flops 4294967296 | bytes 2097152 | tf_op jit(solution)/shard_map/attend/pallas_call | solution.py:397
  29.1 3.7 %finish.1 = (bf16[256,2048]{1,0:T(8,128)(2,1)}, f32[16]{0:T(128)}, bf16[1024,2048]{1,0:T(8,128)(2,1)}, bf16[1024,1024]{1,0:T(8,128)(2,1)}) custom-call(f32[16,144,256]{2,1,0:T(8,128)S(1)} %get-tuple-element.10.acc, f32[1,2048]{1,0:T(1,128)S(1)} %get-tuple-element.11.qf_ref, f32[1,1024]{1,0:T(1,128)S(1)} %get-tuple-element.12.kf_ref, ...), custom_call_target="tpu_custom_call" | custom-call | flops 3145728 | bytes 12582912 | tf_op jit(solution)/shard_map/finish/pallas_call | solution.py:440
